TPU v7x, 32 devices: a 4x4x1 block of a 4x4x8 slice. The times are simulated.
32 devices in a mesh: rep: 1 (over z), tp: 4 (over y), sp: 8 (over x, core).
Axes of the slice: x: 4, y: 4, z: 1, core: 2. Of those that a mesh axis runs over, the one named last changes fastest.
The devices are a block of a 4x4x8 slice.
Arguments:
- x_tokens: bfloat16 [6144, 5120], P(('rep', 'sp'))
- positions: int32 [6144], P(('rep', 'sp'))
- gains: float32 [2, 4, 5120], replicated
- w_q: bfloat16 [2, 5120, 32, 128], P(None, None, 'tp')
- w_k: bfloat16 [2, 5120, 8, 128], P(None, None, 'tp')
- w_v: bfloat16 [2, 5120, 8, 128], P(None, None, 'tp')
- w_o: bfloat16 [2, 32, 128, 5120], P(None, 'tp')
- w_gate: bfloat16 [2, 5120, 14336], P(None, None, 'tp')
- w_up: bfloat16 [2, 5120, 14336], P(None, None, 'tp')
- w_down: bfloat16 [2, 14336, 5120], P(None, 'tp')
Outputs:
- output 1: bfloat16 [6144, 5120], P(('rep', 'sp'))
- output 2: bfloat16 [512, 32, 128], P('rep', ('tp', 'sp'))
- output 3: bfloat16 [512, 32, 128], P('rep', ('tp', 'sp'))
- output 4: bfloat16 [6144, 32, 128], P('rep', ('tp', 'sp'))
- output 5: bfloat16 [6144, 32, 128], P('rep', ('tp', 'sp'))
All inputs are finite; a program needn't handle non-finite values.
Results may differ from a plain program's by a relative error of at most 0.0162716.
Values are sent between devices in bfloat16 or wider.
A program may use at most 768 MiB of HBM per device.

v0:
```python
import jax
import jax.numpy as jnp
from jax import lax
from jax.sharding import PartitionSpec as P, NamedSharding

NORM_EPS = 1e-6
WINDOW = 512
Q_BLOCK = 256
LOCAL_BASE = 10000.0
GLOBAL_BASE = 1000000.0


def rms_norm(values, gain):
    wide = values.astype(jnp.float32)
    inv_rms = lax.rsqrt(jnp.mean(wide * wide, axis=-1, keepdims=True) + NORM_EPS)
    return wide * inv_rms * gain


def rotary(projected, positions, base):
    half = projected.shape[-1] // 2
    inv_freq = base ** (-jnp.arange(half, dtype=jnp.float32) / half)
    angles = positions.astype(jnp.float32)[..., None] * inv_freq
    cos_part = jnp.cos(angles)[..., None, :]
    sin_part = jnp.sin(angles)[..., None, :]
    first = projected[..., :half]
    second = projected[..., half:]
    return jnp.concatenate([first * cos_part - second * sin_part, second * cos_part + first * sin_part], axis=-1)


def attend(q_heads, k_heads, v_heads, q_first, local):
    total = k_heads.shape[0]
    span = WINDOW + Q_BLOCK if local else total
    scale = q_heads.shape[-1] ** -0.5

    def one_block(block_id):
        q_start = block_id * Q_BLOCK
        q_tile = lax.dynamic_slice_in_dim(q_heads, q_start, Q_BLOCK, 0)
        q_idx = q_first + q_start + jnp.arange(Q_BLOCK)
        k_start = jnp.clip(q_first + q_start - WINDOW, 0, total - span) if local else 0
        k_tile = lax.dynamic_slice_in_dim(k_heads, k_start, span, 0)
        v_tile = lax.dynamic_slice_in_dim(v_heads, k_start, span, 0)
        k_idx = k_start + jnp.arange(span)
        allowed = k_idx[None, :] <= q_idx[:, None]
        if local:
            allowed = allowed & (q_idx[:, None] - k_idx[None, :] < WINDOW)
        scores = jnp.einsum('qhgd,khd->hgqk', q_tile, k_tile, preferred_element_type=jnp.float32) * scale
        weights = jax.nn.softmax(jnp.where(allowed, scores, -1e30), axis=-1).astype(jnp.bfloat16)
        return jnp.einsum('hgqk,khd->qhgd', weights, v_tile, preferred_element_type=jnp.float32).astype(jnp.bfloat16)

    blocks = lax.map(one_block, jnp.arange(q_heads.shape[0] // Q_BLOCK))
    return blocks.reshape(q_heads.shape)


def solution(mesh):
    sp_size = mesh.shape['sp']

    def layer(x_loc, pos_loc, gain, w_q, w_k, w_v, w_o, w_gate, w_up, w_down, local):
        base = LOCAL_BASE if local else GLOBAL_BASE
        u_norm = rms_norm(x_loc, gain[0]).astype(jnp.bfloat16)
        q_rot = rotary(jnp.einsum('td,dhe->the', u_norm, w_q, preferred_element_type=jnp.float32), pos_loc, base).astype(jnp.bfloat16)
        k_rot = rotary(jnp.einsum('td,dhe->the', u_norm, w_k, preferred_element_type=jnp.float32), pos_loc, base).astype(jnp.bfloat16)
        v_new = jnp.einsum('td,dhe->the', u_norm, w_v, preferred_element_type=jnp.float32).astype(jnp.bfloat16)
        seq_dev, heads_tp, head_dim = q_rot.shape
        kv_tp = k_rot.shape[1]
        heads_dev = heads_tp // sp_size
        cache_dev = max(kv_tp // sp_size, 1)
        repeat = sp_size * cache_dev // kv_tp
        outgoing = jnp.concatenate([
            q_rot.reshape(seq_dev, sp_size, heads_dev, head_dim),
            jnp.repeat(k_rot, repeat, axis=1).reshape(seq_dev, sp_size, cache_dev, head_dim),
            jnp.repeat(v_new, repeat, axis=1).reshape(seq_dev, sp_size, cache_dev, head_dim)], axis=2)
        received = lax.all_to_all(outgoing, 'sp', 1, 0, tiled=True)
        total = received.shape[0]
        received = received.reshape(total, heads_dev + 2 * cache_dev, head_dim)
        q_all = received[:, :heads_dev].reshape(total, cache_dev, heads_dev // cache_dev, head_dim)
        k_all = received[:, heads_dev:heads_dev + cache_dev]
        v_all = received[:, heads_dev + cache_dev:]
        attn_out = attend(q_all, k_all, v_all, 0, local).reshape(sp_size, seq_dev, heads_dev, head_dim)
        attn_back = lax.all_to_all(attn_out, 'sp', 0, 2, tiled=True).reshape(seq_dev, heads_tp, head_dim)
        o_sum = lax.psum(jnp.einsum('the,hed->td', attn_back, w_o, preferred_element_type=jnp.float32), 'tp')
        x_mid = (x_loc.astype(jnp.float32) + rms_norm(o_sum, gain[1])).astype(jnp.bfloat16)
        u_mlp = rms_norm(x_mid, gain[2]).astype(jnp.bfloat16)
        gate_pre = jnp.dot(u_mlp, w_gate, preferred_element_type=jnp.float32)
        up_pre = jnp.dot(u_mlp, w_up, preferred_element_type=jnp.float32)
        hidden_act = (jax.nn.silu(gate_pre) * up_pre).astype(jnp.bfloat16)
        m_sum = lax.psum(jnp.dot(hidden_act, w_down, preferred_element_type=jnp.float32), 'tp')
        x_out = (x_mid.astype(jnp.float32) + rms_norm(m_sum, gain[3])).astype(jnp.bfloat16)
        if local:
            return x_out, k_all[total - WINDOW:], v_all[total - WINDOW:]
        return x_out, k_all, v_all

    def device_fn(x_loc, pos_loc, gains, w_q, w_k, w_v, w_o, w_gate, w_up, w_down):
        hidden, k_local, v_local = layer(x_loc, pos_loc, gains[0], w_q[0], w_k[0], w_v[0], w_o[0], w_gate[0], w_up[0], w_down[0], True)
        out_hidden, k_global, v_global = layer(hidden, pos_loc, gains[1], w_q[1], w_k[1], w_v[1], w_o[1], w_gate[1], w_up[1], w_down[1], False)
        return out_hidden, k_local, v_local, k_global, v_global

    token_spec = P(('rep', 'sp'), None)
    cache_spec = P('rep', ('tp', 'sp'), None)
    in_specs = (token_spec, P(('rep', 'sp')), P(), P(None, None, 'tp', None), P(None, None, 'tp', None),
                P(None, None, 'tp', None), P(None, 'tp', None, None), P(None, None, 'tp'), P(None, None, 'tp'),
                P(None, 'tp', None))
    out_specs = (token_spec, cache_spec, cache_spec, cache_spec, cache_spec)
    return jax.shard_map(device_fn, mesh=mesh, in_specs=in_specs, out_specs=out_specs, check_vma=False)
```

profile of v0, /device:TPU:97, one launch (start us, length us, event | category | flops | bytes accessed | tf_op | source)
XLA Modules:
  0.0 1960.3 jit_solution(13389323745976711233)
XLA Ops:
  23.3 7.8 fusion.128
  39.5 15.7 fusion.126
  55.2 14.3 copy.59
  69.5 12.5 fusion.119
  94.9 54.3 %all-to-all-done = bf16[768,8,3,128]{0,3,2,1:T(8,128)(2,1)} async-done(((bf16[768,8,3,128]{0,3,2,1:T(8,128)(2,1)}), bf16[768,8,3,128]{0,3,2,1:T(8,128)(2,1)}, u32[]{:S(2)}, u32[]{:S(2)}) %all-to-all-start) | async-done | bytes 4718624 | tf_op jit(solution)/shard_map/all_to_all | solution.py:72
  149.2 6.7 copy.48
  159.7 91.8 %while.22 = (s32[]{:T(128)}, bf16[24,256,1,1,128]{4,1,0,3,2:T(8,128)(2,1)}, s32[24]{0:T(128)S(1)}, bf16[6144,1,128]{2,0,1:T(8,128)(2,1)}, bf16[6144,1,128]{2,0,1...) while((s32[]{:T(128)}, ...), condition=%wide.region_4.5_spmd, body=%wide.region_1.4_spmd.sunk | while | flops 103055880 | bytes 3160307 | solution.py:50
  251.5 25.0 %all_to_all.60 = bf16[8,768,1,128]{3,1,2,0:T(8,128)(2,1)S(1)} all-to-all(bf16[8,768,1,128]{3,1,2,0:T(8,128)(2,1)} %bitcast.246), channel_id=1, replica_groups=mesh['rep'=1,'tp'=4,'sp'=8] {'sp'}, dimensions={0} | all-to-all | bytes 3145728 | tf_op jit(solution)/shard_map/all_to_all | solution.py:79
  276.4 13.6 fusion.79
  290.2 274.2 %all-reduce.5.cloned.1.call-done = f32[768,5120]{1,0:T(8,128)} async-done(((f32[768,5120]{1,0:T(8,128)}), f32[768,5120]{1,0:T(8,128)}) %all-reduce.5.cloned.1.call-update) | async-done | bytes 15728656 | tf_op jit(solution)/shard_map/psum | solution.py:80
  564.4 6.6 multiply_reduce_fusion.3
  571.0 9.5 fusion.61
  580.6 36.6 %fusion.49 = f32[768,3584]{1,0:T(8,128)} fusion(bf16[2,5120,3584]{2,1,0:T(8,128)(2,1)} %param.21, bf16[768,5120]{1,0:T(8,128)(2,1)S(1)} %get-tuple-element.169, f32[5120]{0:T(1024)S(1)} %bitcast.258, f32[768]{0:T(1024)S(1)} %add_rsqrt_fusion.5), kind=kOutput, calls=%fused_computation.50 | convolution fusion | flops 28201451520 | bytes 55598080 | tf_op jit(solution)/shard_map/dot_general | solution.py:83
  617.2 34.3 %multiply_convert_fusion.1 = bf16[768,3584]{1,0:T(8,128)(2,1)S(1)} fusion(f32[768,3584]{1,0:T(8,128)} %fusion.49, bf16[2,5120,3584]{2,1,0:T(8,128)(2,1)} %param.22, bf16[768,5120]{1,0:T(8,128)(2,1)S(1)} %get-tuple-element.169, f32[5120]{0:T(1024)S(1)} %bitcast.259, f32[768]{0:T(1024)S(1)} %add_rsqrt_fusion.5), kind=kOutput, calls=%fused_computation.91 | convolution fusion | flops 28217966592 | bytes 61103104 | tf_op jit(solution)/shard_map/dot_general | solution.py:84
  651.5 34.0 %fusion.45 = f32[768,5120]{1,0:T(8,128)} fusion(bf16[768,3584]{1,0:T(8,128)(2,1)S(1)} %multiply_convert_fusion.1, bf16[2,3584,5120]{2,1,0:T(8,128)(2,1)} %param.23), kind=kOutput, calls=%fused_computation.46 | convolution fusion | flops 28185722880 | bytes 57933824 | tf_op jit(solution)/shard_map/dot_general | solution.py:86
  692.0 24.3 %copy.62 = bf16[1,5120,8,128]{1,3,2,0:T(8,128)(2,1)} copy(bf16[1,5120,8,128]{3,2,1,0:T(8,128)(2,1)} %get-tuple-element.174) | data formatting | bytes 20971520
  716.3 242.8 %all-reduce.7.cloned.1.call-done = f32[768,5120]{1,0:T(8,128)} async-done(((f32[768,5120]{1,0:T(8,128)}), f32[768,5120]{1,0:T(8,128)}) %all-reduce.7.cloned.1.call-update) | async-done | bytes 15728656 | tf_op jit(solution)/shard_map/psum | solution.py:86
  959.1 6.7 multiply_reduce_fusion.2
  965.9 10.4 fusion.65
  976.3 8.5 fusion.114
  1006.7 54.3 %all-to-all-done.2 = bf16[768,8,3,128]{0,3,2,1:T(8,128)(2,1)} async-done(((bf16[768,8,3,128]{0,3,2,1:T(8,128)(2,1)}), bf16[768,8,3,128]{0,3,2,1:T(8,128)(2,1)}, u32[]{:S(2)}, u32[]{:S(2)}) %all-to-all-start.2) | async-done | bytes 4718624 | tf_op jit(solution)/shard_map/all_to_all | solution.py:72
  1061.0 6.9 copy.56
  1071.7 157.6 %while.23 = (s32[]{:T(128)}, bf16[24,256,1,1,128]{4,1,3,2,0:T(8,128)(2,1)}, s32[24]{0:T(128)S(1)}, bf16[6144,1,1,128]{3,0,2,1:T(8,128)(2,1)}, bf16[6144,1,128]{2...) while((s32[]{:T(128)}, ...), condition=%wide.region_14.15_spmd, body=%wide.region_11.14_spmd.sunk | while | flops 819494656 | bytes 22158516 | solution.py:50
  1229.4 25.0 %all_to_all.61 = bf16[8,768,1,128]{3,1,2,0:T(8,128)(2,1)S(1)} all-to-all(bf16[8,768,1,128]{3,1,2,0:T(8,128)(2,1)} %bitcast.245), channel_id=1, replica_groups=mesh['rep'=1,'tp'=4,'sp'=8] {'sp'}, dimensions={0} | all-to-all | bytes 3145728 | tf_op jit(solution)/shard_map/all_to_all | solution.py:79
  1254.3 13.6 fusion.82
  1268.1 271.9 %all-reduce.9.cloned.1.call-done = f32[768,5120]{1,0:T(8,128)} async-done(((f32[768,5120]{1,0:T(8,128)}), f32[768,5120]{1,0:T(8,128)}) %all-reduce.9.cloned.1.call-update) | async-done | bytes 15728656 | tf_op jit(solution)/shard_map/psum | solution.py:80
  1546.6 9.8 fusion.69
  1556.4 36.6 %fusion.43 = f32[768,3584]{1,0:T(8,128)} fusion(bf16[2,5120,3584]{2,1,0:T(8,128)(2,1)} %param.21, bf16[768,5120]{1,0:T(8,128)(2,1)S(1)} %get-tuple-element.165, f32[5120]{0:T(1024)S(1)} %bitcast.253, f32[768]{0:T(1024)S(1)} %add_rsqrt_fusion.1), kind=kOutput, calls=%fused_computation.44 | convolution fusion | flops 28201451520 | bytes 55598080 | tf_op jit(solution)/shard_map/dot_general | solution.py:83
  1593.0 34.3 %multiply_convert_fusion = bf16[768,3584]{1,0:T(8,128)(2,1)S(1)} fusion(f32[768,3584]{1,0:T(8,128)} %fusion.43, bf16[2,5120,3584]{2,1,0:T(8,128)(2,1)} %param.22, bf16[768,5120]{1,0:T(8,128)(2,1)S(1)} %get-tuple-element.165, f32[5120]{0:T(1024)S(1)} %bitcast.254, f32[768]{0:T(1024)S(1)} %add_rsqrt_fusion.1), kind=kOutput, calls=%fused_computation.90 | convolution fusion | flops 28217966592 | bytes 61103104 | tf_op jit(solution)/shard_map/dot_general | solution.py:84
  1627.3 34.4 %fusion.39 = f32[768,5120]{1,0:T(8,128)} fusion(bf16[768,3584]{1,0:T(8,128)(2,1)S(1)} %multiply_convert_fusion, bf16[2,3584,5120]{2,1,0:T(8,128)(2,1)} %param.23), kind=kOutput, calls=%fused_computation.40 | convolution fusion | flops 28185722880 | bytes 57933824 | tf_op jit(solution)/shard_map/dot_general | solution.py:86
  1663.4 271.9 %all-reduce.11.cloned.1.call-done = f32[768,5120]{1,0:T(8,128)} async-done(((f32[768,5120]{1,0:T(8,128)}), f32[768,5120]{1,0:T(8,128)}) %all-reduce.11.cloned.1.call-update) | async-done | bytes 15728656 | tf_op jit(solution)/shard_map/psum | solution.py:86
  1941.9 11.3 fusion.72
  (413 shorter events, 305.4 us)
Async XLA Ops:
  7.2 6.2 copy-start.11
  7.2 6.9 copy-start.4
  23.3 7.8 copy-start.6
  23.3 13.6 slice-start
  31.1 5.8 slice-start.1
  88.4 60.8 %all-to-all-start = ((bf16[768,8,3,128]{0,3,2,1:T(8,128)(2,1)}), bf16[768,8,3,128]{0,3,2,1:T(8,128)(2,1)}, u32[]{:S(2)}, u32[]{:S(2)}) async-start(bf16[768,8,3,128]{0,3,2,1:T(8,128)(2,1)} %copy.47), calls=%async_computation | async-start | bytes 9437184 | tf_op jit(solution)/shard_map/all_to_all | solution.py:72
  94.9 469.5 %all-reduce.5.cloned.1.call-start = ((), (), s32[]{:S(2)}) async-start(), calls=%async_computation.4 | async-start | bytes 31457280 | tf_op jit(solution)/shard_map/psum | solution.py:80
  290.1 669.0 %all-reduce.7.cloned.1.call-start = ((), (), s32[]{:S(2)}) async-start(), calls=%async_computation.5 | async-start | bytes 31457280 | tf_op jit(solution)/shard_map/psum | solution.py:86
  580.5 36.6 %copy-start.1 = (bf16[768,5120]{1,0:T(8,128)(2,1)}, bf16[768,5120]{1,0:T(8,128)(2,1)S(1)}, u32[]{:S(2)}) copy-start(bf16[768,5120]{1,0:T(8,128)(2,1)S(1)} %get-tuple-element.169) | copy-start | bytes 23592964
  685.4 1.7 copy-start.3
  716.3 249.6 %copy-start.14 = (f32[1,1,5120]{2,1,0:T(1,128)S(1)}, f32[1,1,5120]{2,1,0:T(1,128)}, u32[]{:S(2)}) copy-start(f32[1,1,5120]{2,1,0:T(1,128)} %get-tuple-element.199) | copy-start | bytes 61444
  959.1 17.2 slice-start.2
  965.9 10.5 slice-start.3
  965.9 10.5 slice-start.4
  965.9 10.5 copy-start.16
  976.3 13.6 copy-start
  984.8 5.0 copy-start.5
  989.8 5.5 copy-start.7
  989.8 5.5 copy-start.8
  1001.3 59.7 %all-to-all-start.2 = ((bf16[768,8,3,128]{0,3,2,1:T(8,128)(2,1)}), bf16[768,8,3,128]{0,3,2,1:T(8,128)(2,1)}, u32[]{:S(2)}, u32[]{:S(2)}) async-start(bf16[768,8,3,128]{0,3,2,1:T(8,128)(2,1)} %copy.55), calls=%async_computation.2 | async-start | bytes 9437184 | tf_op jit(solution)/shard_map/all_to_all | solution.py:72
  1006.7 533.3 %all-reduce.9.cloned.1.call-start = ((), (), s32[]{:S(2)}) async-start(), calls=%async_computation.6 | async-start | bytes 31457280 | tf_op jit(solution)/shard_map/psum | solution.py:80
  1229.3 38.6 %copy-start.9 = (bf16[6144,1,128]{2,0,1:T(8,128)(2,1)}, bf16[6144,1,128]{2,0,1:T(8,128)(2,1)S(1)}, u32[]{:S(2)}) copy-start(bf16[6144,1,128]{2,0,1:T(8,128)(2,1)S(1)} %get-tuple-element.380) | copy-start | bytes 4718596
  1229.4 38.6 %copy-start.10 = (bf16[6144,1,128]{2,0,1:T(8,128)(2,1)}, bf16[6144,1,128]{2,0,1:T(8,128)(2,1)S(1)}, u32[]{:S(2)}) copy-start(bf16[6144,1,128]{2,0,1:T(8,128)(2,1)S(1)} %get-tuple-element.381) | copy-start | bytes 4718596
  1268.0 278.6 %copy-start.13 = (f32[1,1,5120]{2,1,0:T(1,128)S(1)}, f32[1,1,5120]{2,1,0:T(1,128)}, u32[]{:S(2)}) copy-start(f32[1,1,5120]{2,1,0:T(1,128)} %get-tuple-element.197) | copy-start | bytes 61444
  1268.0 667.3 %all-reduce.11.cloned.1.call-start = ((), (), s32[]{:S(2)}) async-start(), calls=%async_computation.7 | async-start | bytes 31457280 | tf_op jit(solution)/shard_map/psum | solution.py:86
  1546.6 9.8 copy-start.15
  1556.4 36.6 %copy-start.2 = (bf16[768,5120]{1,0:T(8,128)(2,1)}, bf16[768,5120]{1,0:T(8,128)(2,1)S(1)}, u32[]{:S(2)}) copy-start(bf16[768,5120]{1,0:T(8,128)(2,1)S(1)} %get-tuple-element.165) | copy-start | bytes 23592964
  1663.4 278.5 %copy-start.12 = (f32[1,1,5120]{2,1,0:T(1,128)S(1)}, f32[1,1,5120]{2,1,0:T(1,128)}, u32[]{:S(2)}) copy-start(f32[1,1,5120]{2,1,0:T(1,128)} %get-tuple-element.196) | copy-start | bytes 61444
Sparse Core Ops, SparseCore 0:
  290.2 274.1 all-reduce.4
  685.6 273.4 all-reduce.6
  1268.1 271.8 all-reduce.8
  1661.8 273.4 all-reduce.10
where the time goes:
time: 1970 us; the launch traced here: 1960 us
  waiting for transfers between devices  1170 us (59%)
  matrix products  417 us (21%)
  local copies, waits for them, and re-layouts  156 us (8%)
  other arithmetic  108 us (5%)
  blocking collectives  50 us (3%)
  loops' own time  32.6 us (2%)
    psum x2, waiting for transfers between devices, layer(): lax.psum(jnp.einsum('the,hed->td', attn_back, w_o, preferred_element_type...  546 us
    psum x2, waiting for transfers between devices, layer(): lax.psum(jnp.dot(hidden_act, w_down, preferred_element_type=jnp.float32),...  515 us
    all_to_all x2, waiting for transfers between devices, layer(): received = lax.all_to_all(outgoing, 'sp', 1, 0, tiled=True)  109 us
    dot_general x48, matrix products, one_block(): jnp.einsum('hgqk,khd->qhgd', weights, v_tile, preferred_element_type=jnp....  81 us
    dot_general x2, matrix products, layer(): gate_pre = jnp.dot(u_mlp, w_gate, preferred_element_type=jnp.float32)  73.2 us
    dot_general x2, matrix products, layer(): up_pre = jnp.dot(u_mlp, w_up, preferred_element_type=jnp.float32)  68.6 us
    dot_general x2, matrix products, layer(): jnp.dot(hidden_act, w_down, preferred_element_type=jnp.float32)  68.3 us
    reduce_sum x8, other arithmetic, rms_norm(): jnp.mean(wide * wide, axis=-1, keepdims=True) + NORM_EPS  61.4 us
  transfers between devices with their start and end apart: 6, of which 6 were waited for; matrix products, arithmetic and copies ran while one was open for 2% of the time, Pallas kernels for 0%

commit v1 on v0

v1 whole, which is shorter than its diff:
```python
import functools
import math

import jax
import jax.numpy as jnp
from jax import lax
from jax.experimental import pallas as pl
from jax.experimental.pallas import tpu as pltpu
from jax.sharding import PartitionSpec as P


NORM_EPS = 1e-6
WINDOW = 512
Q_BLOCK = 256
LOCAL_BASE = 10000.0
GLOBAL_BASE = 1000000.0
CHUNKS = 2
F32 = jnp.float32
BF16 = jnp.bfloat16
NEG = -1e30


def rms_norm(values, gain):
    wide = values.astype(F32)
    inv_rms = lax.rsqrt(jnp.mean(wide * wide, axis=-1, keepdims=True) + NORM_EPS)
    return wide * inv_rms * gain


def rope_tables(positions, half, base):
    inv_freq = base ** (-jnp.arange(half, dtype=F32) / half)
    angles = positions.astype(F32)[:, None] * inv_freq
    cos, sin = jnp.cos(angles), jnp.sin(angles)
    return jnp.concatenate([cos, cos], axis=1), jnp.concatenate([-sin, sin], axis=1)


def rotate(x, cos, sin):
    return (x * cos + pltpu.roll(x, x.shape[-1] // 2, 1) * sin).astype(BF16)


def rope_local_kernel(q_ref, k_ref, v_ref, cos_ref, sin_ref, qo_ref, ko_ref, vo_ref):
    head_dim = cos_ref.shape[1]
    cos, sin = cos_ref[...], sin_ref[...]
    for h in range(qo_ref.shape[0]):
        qo_ref[h] = rotate(q_ref[:, h * head_dim:(h + 1) * head_dim], cos, sin)
    for h in range(ko_ref.shape[0]):
        ko_ref[h] = rotate(k_ref[:, h * head_dim:(h + 1) * head_dim], cos, sin)
        vo_ref[h] = v_ref[:, h * head_dim:(h + 1) * head_dim].astype(BF16)


def rope_local(q, k, v, cos, sin):
    tokens, head_dim = cos.shape
    n_q, n_k = q.shape[1] // head_dim, k.shape[1] // head_dim
    return pl.pallas_call(
        rope_local_kernel,
        out_shape=[jax.ShapeDtypeStruct((n, tokens, head_dim), BF16) for n in (n_q, n_k, n_k)],
        cost_estimate=pl.CostEstimate(flops=4 * q.size, bytes_accessed=8 * q.size, transcendentals=0),
        name='rope_local',
    )(q, k, v, cos, sin)


def rope_send_kernel(repeat, q_ref, k_ref, v_ref, cos_ref, sin_ref, out_ref):
    head_dim = cos_ref.shape[1]
    cos, sin = cos_ref[...], sin_ref[...]
    n_q = out_ref.shape[0]
    for h in range(n_q):
        out_ref[h, 0] = rotate(q_ref[:, h * head_dim:(h + 1) * head_dim], cos, sin)
    for g in range(n_q // repeat):
        k = rotate(k_ref[:, g * head_dim:(g + 1) * head_dim], cos, sin)
        v = v_ref[:, g * head_dim:(g + 1) * head_dim].astype(BF16)
        for h in range(g * repeat, (g + 1) * repeat):
            out_ref[h, 1] = k
            out_ref[h, 2] = v


def rope_send(q, k, v, cos, sin):
    tokens, head_dim = cos.shape
    n_q, n_k = q.shape[1] // head_dim, k.shape[1] // head_dim
    return pl.pallas_call(
        functools.partial(rope_send_kernel, n_q // n_k),
        out_shape=jax.ShapeDtypeStruct((n_q, 3, tokens, head_dim), BF16),
        cost_estimate=pl.CostEstimate(flops=4 * q.size, bytes_accessed=12 * q.size, transcendentals=0),
        name='rope_send',
    )(q, k, v, cos, sin)


def local_kernel(scale, first_ref, q_ref, k_ref, v_ref, o_ref):
    block = pl.program_id(1)
    group, rows, _ = q_ref.shape
    span = WINDOW + rows
    start = pl.multiple_of(block * rows, rows)
    k = k_ref[0, pl.ds(start, span), :]
    v = v_ref[0, pl.ds(start, span), :]
    r = lax.broadcasted_iota(jnp.int32, (rows, span), 0)
    j = lax.broadcasted_iota(jnp.int32, (rows, span), 1)
    lowest = WINDOW - start - first_ref[0]
    allowed = (j <= r + WINDOW) & (j > r) & (j >= lowest)
    for h in range(group):
        s = lax.dot_general(q_ref[h], k, (((1,), (1,)), ((), ())), preferred_element_type=F32) * scale
        s = jnp.where(allowed, s, NEG)
        p = jnp.exp2(s - jnp.max(s, axis=1, keepdims=True))
        total = jnp.sum(p, axis=1, keepdims=True)
        out = jnp.dot(p.astype(BF16), v, preferred_element_type=F32) / total
        o_ref[h] = out.astype(BF16)


def local_attention(q, k_ext, v_ext, first):
    n_q, tokens, head_dim = q.shape
    n_k = k_ext.shape[0]
    group = n_q // n_k
    scale = math.log2(math.e) * head_dim ** -0.5
    flops = 4 * n_q * tokens * (WINDOW + Q_BLOCK) * head_dim
    return pl.pallas_call(
        functools.partial(local_kernel, scale),
        grid_spec=pltpu.PrefetchScalarGridSpec(
            num_scalar_prefetch=1,
            grid=(n_k, tokens // Q_BLOCK),
            in_specs=[
                pl.BlockSpec((group, Q_BLOCK, head_dim), lambda g, b, s: (g, b, 0)),
                pl.BlockSpec((1, k_ext.shape[1], head_dim), lambda g, b, s: (g, 0, 0)),
                pl.BlockSpec((1, k_ext.shape[1], head_dim), lambda g, b, s: (g, 0, 0)),
            ],
            out_specs=pl.BlockSpec((group, Q_BLOCK, head_dim), lambda g, b, s: (g, b, 0)),
        ),
        out_shape=jax.ShapeDtypeStruct((n_q, tokens, head_dim), BF16),
        cost_estimate=pl.CostEstimate(flops=2 * flops, bytes_accessed=4 * q.size, transcendentals=flops // (4 * head_dim)),
        name='local_attention',
    )(first, q, k_ext, v_ext)


def global_kernel(scale, offset, q_ref, k_ref, v_ref, o_ref, acc_ref, m_ref, l_ref):
    src = pl.program_id(0)
    q = q_ref[0, 0]
    rows = q.shape[0]

    def scores(k):
        return lax.dot_general(q, k, (((1,), (1,)), ((), ())), preferred_element_type=F32) * scale

    width = offset + rows
    s = scores(k_ref[src, :width])
    r = lax.broadcasted_iota(jnp.int32, (rows, width), 0)
    j = lax.broadcasted_iota(jnp.int32, (rows, width), 1)
    s = jnp.where(j <= r + offset, s, NEG)
    m = jnp.max(s, axis=1, keepdims=True)
    p = jnp.exp2(s - m)
    m_ref[...] = m
    l_ref[...] = jnp.sum(p, axis=1, keepdims=True)
    acc_ref[...] = jnp.dot(p.astype(BF16), v_ref[src, :width], preferred_element_type=F32)

    def step(i, _):
        s = scores(k_ref[i])
        m_old = m_ref[...]
        m_new = jnp.maximum(m_old, jnp.max(s, axis=1, keepdims=True))
        p = jnp.exp2(s - m_new)
        alpha = jnp.exp2(m_old - m_new)
        m_ref[...] = m_new
        l_ref[...] = l_ref[...] * alpha + jnp.sum(p, axis=1, keepdims=True)
        acc_ref[...] = acc_ref[...] * alpha + jnp.dot(p.astype(BF16), v_ref[i], preferred_element_type=F32)
        return 0

    lax.fori_loop(0, src, step, 0)
    o_ref[0] = (acc_ref[...] / l_ref[...]).astype(BF16)


def global_attention(received, k_all, v_all, offset):
    n_src, _, rows, head_dim = received.shape
    scale = math.log2(math.e) * head_dim ** -0.5
    total = k_all.shape[0] * k_all.shape[1]
    flops = 2 * n_src * rows * total * head_dim
    return pl.pallas_call(
        functools.partial(global_kernel, scale, offset),
        grid=(n_src,),
        in_specs=[
            pl.BlockSpec((1, 1, rows, head_dim), lambda s: (s, 0, 0, 0)),
            pl.BlockSpec(k_all.shape, lambda s: (0, 0, 0)),
            pl.BlockSpec(k_all.shape, lambda s: (0, 0, 0)),
        ],
        out_specs=pl.BlockSpec((1, rows, head_dim), lambda s: (s, 0, 0)),
        out_shape=jax.ShapeDtypeStruct((n_src, rows, head_dim), BF16),
        scratch_shapes=[pltpu.VMEM((rows, head_dim), F32), pltpu.VMEM((rows, 1), F32), pltpu.VMEM((rows, 1), F32)],
        cost_estimate=pl.CostEstimate(flops=2 * flops, bytes_accessed=8 * total * head_dim, transcendentals=flops // (4 * head_dim)),
        name='global_attention',
    )(received, k_all, v_all)


def normed(wide, gain):
    mean = jnp.mean(wide * wide, axis=1, keepdims=True)
    return wide * lax.rsqrt(mean + NORM_EPS) * gain


def joined(ref):
    return jnp.concatenate([ref[i] for i in range(ref.shape[0])], axis=1)


def norm_kernel(h_ref, gain_ref, u_ref):
    u_ref[...] = normed(joined(h_ref).astype(F32), gain_ref[...]).astype(BF16)


def norm_columns(h, gain):
    n, rows, columns = h.shape
    width, block = n * columns, 64
    return pl.pallas_call(
        norm_kernel,
        grid=(rows // block,),
        in_specs=[
            pl.BlockSpec((n, block, columns), lambda i: (0, i, 0)),
            pl.BlockSpec((1, width), lambda i: (0, 0)),
        ],
        out_specs=pl.BlockSpec((block, width), lambda i: (i, 0)),
        out_shape=jax.ShapeDtypeStruct((rows, width), BF16),
        cost_estimate=pl.CostEstimate(flops=6 * h.size, bytes_accessed=4 * h.size, transcendentals=rows),
        name='norm_columns',
    )(h, gain.reshape(1, width))


def finish_kernel(id_ref, h_ref, sum_ref, gain_ref, o_ref):
    del id_ref
    o_ref[...] = (joined(h_ref).astype(F32) + normed(sum_ref[...], gain_ref[...])).astype(BF16)


def finish(ids, h, total, gain):
    rows, width = total.shape
    n, _, columns = h.shape
    block = 32
    steps = rows // block
    return pl.pallas_call(
        finish_kernel,
        grid_spec=pltpu.PrefetchScalarGridSpec(
            num_scalar_prefetch=1,
            grid=(steps,),
            in_specs=[
                pl.BlockSpec((n, block, columns), lambda i, s: (0, s[0] * steps + i, 0)),
                pl.BlockSpec((block, width), lambda i, s: (i, 0)),
                pl.BlockSpec((1, width), lambda i, s: (0, 0)),
            ],
            out_specs=pl.BlockSpec((block, width), lambda i, s: (i, 0)),
        ),
        out_shape=jax.ShapeDtypeStruct((rows, width), BF16),
        cost_estimate=pl.CostEstimate(flops=8 * total.size, bytes_accessed=8 * total.size, transcendentals=rows),
        name='finish',
    )(ids, h, total, gain.reshape(1, width))


def output_kernel(id_ref, a_ref, w_ref, o_ref):
    del id_ref
    w = w_ref[...].reshape(w_ref.shape[0] * w_ref.shape[2], w_ref.shape[3])
    part = jnp.dot(joined(a_ref.at[0]), w, preferred_element_type=F32)

    @pl.when(pl.program_id(0) == 0)
    def _():
        o_ref[...] = part

    @pl.when(pl.program_id(0) > 0)
    def _():
        o_ref[...] += part


def output_projection(ids, attn, w):
    tp, heads, rows, head_dim = attn.shape
    columns = w.shape[3]
    return pl.pallas_call(
        output_kernel,
        grid_spec=pltpu.PrefetchScalarGridSpec(
            num_scalar_prefetch=1,
            grid=(tp,),
            in_specs=[
                pl.BlockSpec((1, heads, rows, head_dim), lambda k, s: (lax.rem(s[0] + tp - k, tp), 0, 0, 0)),
                pl.BlockSpec((heads, 1, head_dim, columns), lambda k, s: (0, k, 0, 0)),
            ],
            out_specs=pl.BlockSpec((rows, columns), lambda k, s: (0, 0)),
        ),
        out_shape=jax.ShapeDtypeStruct((rows, columns), F32),
        cost_estimate=pl.CostEstimate(flops=2 * attn.size * columns, bytes_accessed=2 * attn.size + 2 * w.size + 4 * rows * columns, transcendentals=0),
        name='output_projection',
    )(ids, attn, w)


def add_columns_kernel(width, id_ref, x_ref, o_ref, square_ref, gain_ref, h_ref):
    del id_ref
    inv_rms = lax.rsqrt(square_ref[...] / width + NORM_EPS)
    h_ref[...] = (x_ref[...].astype(F32) + o_ref[...] * inv_rms * gain_ref[...]).astype(BF16)


def add_columns(ids, x, first_row, o, squares, gain):
    rows, columns = o.shape
    width = x.shape[1]
    block = 128
    first_block = first_row // block
    return pl.pallas_call(
        functools.partial(add_columns_kernel, width),
        grid_spec=pltpu.PrefetchScalarGridSpec(
            num_scalar_prefetch=1,
            grid=(rows // block,),
            in_specs=[
                pl.BlockSpec((block, columns), lambda i, s: (first_block + i, s[0])),
                pl.BlockSpec((block, columns), lambda i, s: (i, 0)),
                pl.BlockSpec((block, 1), lambda i, s: (i, 0)),
                pl.BlockSpec((1, columns), lambda i, s: (0, s[0])),
            ],
            out_specs=pl.BlockSpec((block, columns), lambda i, s: (i, 0)),
        ),
        out_shape=jax.ShapeDtypeStruct((rows, columns), BF16),
        cost_estimate=pl.CostEstimate(flops=6 * o.size, bytes_accessed=8 * o.size, transcendentals=rows),
        name='add_columns',
    )(ids, x, o, squares.reshape(rows, 1), gain.reshape(1, width))


def dot(a, b):
    return jnp.dot(a, b, preferred_element_type=F32)


def solution(mesh):
    sp_size = mesh.shape['sp']
    tp_size = mesh.shape['tp']

    def device_fn(x_loc, pos_loc, gains, w_q, w_k, w_v, w_o, w_gate, w_up, w_down):
        seq, width = x_loc.shape
        heads_tp, head_dim = w_q.shape[2:]
        kv_tp = w_k.shape[2]
        share = sp_size // kv_tp
        sp_id = lax.axis_index('sp')
        tp_id = lax.axis_index('tp')
        rows = seq // CHUNKS

        def project(u, weights, l):
            return tuple(dot(u, w[l].reshape(width, -1)) for w in weights)

        def scatter(partial):
            return lax.psum_scatter(partial, 'tp', scatter_dimension=0, tiled=True)

        def gather(shard):
            return lax.all_gather(shard, 'tp', axis=0, tiled=True)

        ids = tp_id.astype(jnp.int32).reshape(1)
        columns = width // tp_size
        heads_dev = heads_tp // sp_size

        def spread(l):
            blocks = []
            for k in range(tp_size):
                target = lax.rem(tp_id + k, tp_size)
                block = lax.dynamic_slice(w_o, (l, sp_id * heads_dev, 0, target * columns), (1, heads_dev, head_dim, columns))[0]
                if k:
                    block = lax.ppermute(block, 'tp', [(i, (i + k) % tp_size) for i in range(tp_size)])
                blocks.append(block)
            return jnp.stack(blocks, axis=1)

        def collect(blocks):
            return lax.all_gather(blocks, 'sp', axis=0, tiled=True)

        def attn_tail(x, first_row, attn, w_columns, l, after):
            attn = lax.all_gather(attn, 'tp', axis=0)
            attn, _ = lax.optimization_barrier((attn, after[0]))
            o_sum = output_projection(ids, attn, w_columns)
            squares = lax.psum(jnp.sum(o_sum * o_sum, axis=1), 'tp')
            h1 = mine = add_columns(ids, x, first_row, o_sum, squares, gains[l, 1])
            h1 = lax.all_gather(h1, 'tp', axis=0)
            h1, _ = lax.optimization_barrier((h1, after[1]))
            u2 = norm_columns(h1, gains[l, 2])
            act = (jax.nn.silu(dot(u2, w_gate[l])) * dot(u2, w_up[l])).astype(BF16)
            m_part = dot(act, w_down[l])
            m_sum = scatter(m_part)
            out = finish(ids, h1, m_sum, gains[l, 3])
            out = gather(out)
            return out, (mine, m_part)

        u = rms_norm(x_loc, gains[0, 0]).astype(BF16)
        cos, sin = rope_tables(pos_loc, head_dim // 2, LOCAL_BASE)
        q, k, v = rope_local(*project(u, (w_q, w_k, w_v), 0), cos, sin)
        blocks = [spread(0), spread(1)]
        q, k, v, blocks = lax.optimization_barrier((q, k, v, blocks))
        tail = jnp.stack([k[:, seq - WINDOW:], v[:, seq - WINDOW:]])
        halo = lax.ppermute(tail, 'sp', [(i, i + 1) for i in range(sp_size - 1)])
        k_ext = jnp.concatenate([halo[0], k], axis=1)
        v_ext = jnp.concatenate([halo[1], v], axis=1)
        first = (sp_id * seq).astype(jnp.int32).reshape(1)
        w_columns = collect(blocks[0])
        attn = local_attention(q, k_ext, v_ext, first)
        tails = lax.all_gather(tail, 'sp', axis=0)[sp_size - 1]
        cache = lax.dynamic_index_in_dim(tails, sp_id // share, 1, keepdims=False)
        attn, cache, w_columns = lax.optimization_barrier((attn, cache, w_columns))
        later, attn = lax.optimization_barrier(((w_q, w_k, w_v), attn))

        cos, sin = rope_tables(pos_loc, head_dim // 2, GLOBAL_BASE)
        outs, received, after = [], [], (first, first)
        for c in range(CHUNKS):
            part = slice(c * rows, (c + 1) * rows)
            out, after = attn_tail(x_loc, c * rows, attn[:, part], w_columns, 0, after)
            if c:
                out, _ = lax.optimization_barrier((out, received[-1]))
            u = norm_columns(out[None], gains[1, 0])
            outgoing = rope_send(*project(u, later, 1), cos[part], sin[part])
            outs.append(out)
            received.append(lax.all_to_all(outgoing, 'sp', 0, 0, tiled=True))

        blocks, received[-1] = lax.optimization_barrier((blocks[1], received[-1]))
        w_columns = collect(blocks)
        k_all = jnp.concatenate([r[:, 1] for r in received], axis=1)
        v_all = jnp.concatenate([r[:, 2] for r in received], axis=1)
        finals = []
        for c in range(CHUNKS):
            attn = global_attention(received[c], k_all, v_all, c * rows)
            back = lax.all_to_all(attn, 'sp', 0, 0, tiled=True)
            if c == 0:
                back, w_columns = lax.optimization_barrier((back, w_columns))
            out, after = attn_tail(outs[c], 0, back, w_columns, 1, after)
            finals.append(out)
        hidden = jnp.concatenate(finals, axis=0)
        k_local, v_local = cache[0][:, None, :], cache[1][:, None, :]
        k_global = k_all.reshape(-1, 1, head_dim)
        v_global = v_all.reshape(-1, 1, head_dim)
        return hidden, k_local, v_local, k_global, v_global

    token_spec = P(('rep', 'sp'), None)
    cache_spec = P('rep', ('tp', 'sp'), None)
    in_specs = (token_spec, P(('rep', 'sp')), P(), P(None, None, 'tp', None), P(None, None, 'tp', None),
                P(None, None, 'tp', None), P(None, 'tp', None, None), P(None, None, 'tp'), P(None, None, 'tp'),
                P(None, 'tp', None))
    out_specs = (token_spec, cache_spec, cache_spec, cache_spec, cache_spec)
    return jax.shard_map(device_fn, mesh=mesh, in_specs=in_specs, out_specs=out_specs, check_vma=False)
```

time: 1970 us -> 1300 us (0.66)
  waiting for transfers between devices: 1170 us -> 496 us
  Pallas kernels: 0 us -> 208 us
  local copies, waits for them, and re-layouts: 156 us -> 36.5 us
  blocking collectives: 50 us -> 155 us
  matrix products: 417 us -> 321 us
  other arithmetic: 108 us -> 32.2 us
  loops' own time: 32.6 us -> 0 us
    psum x4 -> x0, waiting for transfers between devices: 1060 us -> none  [the longest x2 546 us: layer(): lax.psum(jnp.einsum('the,hed->td', attn_back, w_o, preferred_element_type...]
    all_gather x0 -> x15, waiting for transfers between devices: none -> 253 us  [the longest x4 122 us: gather(): return lax.all_gather(shard, 'tp', axis=0, tiled=True)]
    reduce_scatter x0 -> x4, waiting for transfers between devices: none -> 217 us  [scatter(): return lax.psum_scatter(partial, 'tp', scatter_dimension=0, tiled=True)]
    pallas_call x0 -> x24, Pallas kernels: none -> 208 us  [the longest x2 73.6 us: global_attention(): pl.pallas_call(functools.partial(global_kernel, scale, offset), grid=(n_s...]
    all_to_all x2 -> x1, waiting for transfers between devices: 109 us -> 13.3 us  [device_fn(): received.append(lax.all_to_all(outgoing, 'sp', 0, 0, tiled=True))]
    psum x0 -> x4, blocking collectives: none -> 81.2 us  [attn_tail(): squares = lax.psum(jnp.sum(o_sum * o_sum, axis=1), 'tp')]
    dot_general x106 -> x21, matrix products: 387 us -> 321 us  [dot(): return jnp.dot(a, b, preferred_element_type=F32)]
    reduce_sum x8 -> x1, other arithmetic: 61.4 us -> 1.6 us  [rms_norm(): jnp.mean(wide * wide, axis=-1, keepdims=True) + NORM_EPS]
  transfers between devices with their start and end apart: 6 -> 27, of which waited for: 6 -> 17; matrix products, arithmetic and copies ran while one was open for 2% -> 22% of each run, Pallas kernels for 0% -> 15%
where the time goes in v1:
time: 1300 us; the launch traced here: 1280 us
  waiting for transfers between devices  496 us (38%)
  matrix products  321 us (25%)
  Pallas kernels  208 us (16%)
  blocking collectives  155 us (12%)
  local copies, waits for them, and re-layouts  36.5 us (3%)
  other arithmetic  32.2 us (2%)
  starting transfers between devices  22.4 us (2%)
  between operations  14.8 us (1%)
    dot_general x21, matrix products, dot(): return jnp.dot(a, b, preferred_element_type=F32)  321 us
    reduce_scatter x4, waiting for transfers between devices, scatter(): return lax.psum_scatter(partial, 'tp', scatter_dimension=0, tiled=True)  217 us
    all_gather x4, waiting for transfers between devices, gather(): return lax.all_gather(shard, 'tp', axis=0, tiled=True)  122 us
    psum x4, blocking collectives, attn_tail(): squares = lax.psum(jnp.sum(o_sum * o_sum, axis=1), 'tp')  81.2 us
    pallas_call x2, Pallas kernels, global_attention(): pl.pallas_call(functools.partial(global_kernel, scale, offset), grid=(n_s...  73.6 us
    all_gather x2, waiting for transfers between devices, collect(): return lax.all_gather(blocks, 'sp', axis=0, tiled=True)  57.3 us
    all_gather x4, waiting for transfers between devices, attn_tail(): attn = lax.all_gather(attn, 'tp', axis=0)  46.5 us
    pallas_call x6, Pallas kernels, norm_columns(): pl.pallas_call(norm_kernel, grid=(rows // block,), in_specs=[pl.BlockSpec...  40.4 us
  transfers between devices with their start and end apart: 27, of which 17 were waited for; matrix products, arithmetic and copies ran while one was open for 22% of the time, Pallas kernels for 15%

profile of v1, /device:TPU:97, one launch (start us, length us, event | category | flops | bytes accessed | tf_op | source)
XLA Modules:
  0.0 1284.7 jit_solution(4237573027386939551)
XLA Ops:
  95.8 56.8 %all-gather.25.cloned.1.call-done.w_ref = bf16[8,4,128,1280]{3,2,1,0:T(8,128)(2,1)} async-done(((bf16[1,4,128,1280]{3,2,1,0:T(8,128)(2,1)}), bf16[8,4,128,1280]{3,2,1,0:T(8,128)(2,1)}) %all-gather.25.cloned.1.call-update) | async-done | bytes 10485776 | tf_op jit(solution)/shard_map/all_gather | solution.py:348
  156.0 36.1 %all-gather.39.cloned.1.call-done = bf16[32,384,128]{2,1,0:T(8,128)(2,1)} async-done(((bf16[8,384,128]{2,1,0:T(8,128)(2,1)}), bf16[32,384,128]{2,1,0:T(8,128)(2,1)}) %all-gather.39.cloned.1.call-update) | async-done | bytes 3145744 | tf_op jit(solution)/shard_map/all_gather | solution.py:351
  203.6 19.9 %psum.28.square_ref = f32[384,1]{1,0:T(8,128)} all-reduce(f32[384,1]{1,0:T(8,128)S(1)} %reshape.75), channel_id=1, replica_groups=mesh['rep'=1,'tp'=4,'sp'=8] {'tp'}, use_global_device_ids=true, to_apply=%region_2.3 | all-reduce | flops 384 | bytes 3072 | tf_op jit(solution)/shard_map/psum | solution.py:354
  245.9 19.8 %psum.29.square_ref = f32[384,1]{1,0:T(8,128)} all-reduce(f32[384,1]{1,0:T(8,128)S(1)} %reshape.76), channel_id=1, replica_groups=mesh['rep'=1,'tp'=4,'sp'=8] {'tp'}, use_global_device_ids=true, to_apply=%region_5.6 | all-reduce | flops 384 | bytes 3072 | tf_op jit(solution)/shard_map/psum | solution.py:354
  269.9 12.8 all-gather.41.cloned.1.call-done
  289.4 23.8 %fusion.22 = f32[384,3584]{1,0:T(8,128)} fusion(bf16[384,5120]{1,0:T(8,128)(2,1)} %norm_columns.6, bf16[2,5120,3584]{2,1,0:T(8,128)(2,1)} %param.17), kind=kOutput, calls=%fused_computation.22 | convolution fusion | flops 14092861440 | bytes 46137344 | tf_op jit(solution)/shard_map/dot_general | solution.py:308
  313.2 22.4 %fusion.75.clone.2 = bf16[384,3584]{1,0:T(8,128)(2,1)} fusion(bf16[384,5120]{1,0:T(8,128)(2,1)S(1)} %copy-done.6, bf16[2,5120,3584]{2,1,0:T(8,128)(2,1)} %param.18, f32[384,3584]{1,0:T(8,128)} %fusion.22), kind=kOutput, calls=%fused_computation.58.clone.clone.clone | convolution fusion | flops 14101118976 | bytes 48889856 | tf_op jit(solution)/shard_map/dot_general | solution.py:308
  335.6 22.8 %fusion.14 = f32[384,5120]{1,0:T(8,128)} fusion(bf16[2,3584,5120]{2,1,0:T(8,128)(2,1)} %param.19, bf16[384,3584]{1,0:T(8,128)(2,1)} %fusion.75.clone.2), kind=kOutput, calls=%fused_computation.14 | convolution fusion | flops 14092861440 | bytes 47316992 | tf_op jit(solution)/shard_map/dot_general | solution.py:308
  365.2 23.2 %fusion.20 = f32[384,3584]{1,0:T(8,128)} fusion(bf16[384,5120]{1,0:T(8,128)(2,1)} %norm_columns.8, bf16[2,5120,3584]{2,1,0:T(8,128)(2,1)} %param.17), kind=kOutput, calls=%fused_computation.20 | convolution fusion | flops 14092861440 | bytes 46137344 | tf_op jit(solution)/shard_map/dot_general | solution.py:308
  388.4 22.4 %fusion.70.clone.5 = bf16[384,3584]{1,0:T(8,128)(2,1)} fusion(bf16[384,5120]{1,0:T(8,128)(2,1)S(1)} %copy-done.3, bf16[2,5120,3584]{2,1,0:T(8,128)(2,1)} %param.18, f32[384,3584]{1,0:T(8,128)} %fusion.20), kind=kOutput, calls=%fused_computation.57.clone.clone.clone.2 | convolution fusion | flops 14101118976 | bytes 48889856 | tf_op jit(solution)/shard_map/dot_general | solution.py:308
  410.8 22.8 %fusion.12 = f32[384,5120]{1,0:T(8,128)} fusion(bf16[2,3584,5120]{2,1,0:T(8,128)(2,1)} %param.19, bf16[384,3584]{1,0:T(8,128)(2,1)} %fusion.70.clone.5), kind=kOutput, calls=%fused_computation.12 | convolution fusion | flops 14092861440 | bytes 47316992 | tf_op jit(solution)/shard_map/dot_general | solution.py:308
  437.9 71.2 %reduce-scatter.7.cloned.1.call-done.sum_ref = f32[96,5120]{1,0:T(8,128)} async-done(((f32[384,5120]{1,0:T(8,128)}), f32[96,5120]{1,0:T(8,128)}) %reduce-scatter.7.cloned.1.call-update) | async-done | bytes 1966096 | tf_op jit(solution)/shard_map/reduce_scatter | solution.py:328
  533.7 20.7 %all-gather.27.cloned.1.call-done.x_ref = bf16[384,5120]{1,0:T(8,128)(2,1)} async-done(((bf16[96,5120]{1,0:T(8,128)(2,1)}), bf16[384,5120]{1,0:T(8,128)(2,1)}) %all-gather.27.cloned.1.call-update) | async-done | bytes 3932176 | tf_op jit(solution)/shard_map/all_gather | solution.py:331
  584.5 15.7 %all-gather.29.cloned.1.call-done.x_ref = bf16[384,5120]{1,0:T(8,128)(2,1)} async-done(((bf16[96,5120]{1,0:T(8,128)(2,1)}), bf16[384,5120]{1,0:T(8,128)(2,1)}) %all-gather.29.cloned.1.call-update) | async-done | bytes 3932176 | tf_op jit(solution)/shard_map/all_gather | solution.py:331
  600.2 13.3 %all-to-all-done.q_ref = bf16[8,3,384,128]{3,2,1,0:T(8,128)(2,1)S(1)} async-done(((bf16[8,3,384,128]{3,2,1,0:T(8,128)(2,1)}), bf16[8,3,384,128]{3,2,1,0:T(8,128)(2,1)S(1)}, u32[]{:S(2)}, u32[]{:S(2)}) %all-to-all-start) | async-done | bytes 2359328 | tf_op jit(solution)/shard_map/all_to_all | solution.py:393
  639.1 34.4 %all_to_all.20.q_ref = bf16[8,3,384,128]{3,2,1,0:T(8,128)(2,1)} all-to-all(bf16[8,3,384,128]{3,2,1,0:T(8,128)(2,1)} %rope_send.3), channel_id=1, replica_groups=mesh['rep'=1,'tp'=4,'sp'=8] {'sp'}, dimensions={0} | all-to-all | bytes 4718592 | tf_op jit(solution)/shard_map/all_to_all | solution.py:393
  678.0 35.3 %global_attention.2 = bf16[8,384,128]{2,1,0:T(8,128)(2,1)} custom-call(bf16[8,3,384,128]{3,2,1,0:T(8,128)(2,1)} %copy-done, bf16[8,768,128]{2,1,0:T(8,128)(2,1)} %pad_maximum_fusion.1.k_ref, bf16[8,768,128]{2,1,0:T(8,128)(2,1)} %pad_maximum_fusion.2.v_ref), custom_call_target="tpu_custom_call" | custom-call | flops 9663676416 | bytes 6291456 | tf_op jit(solution)/shard_map/global_attention/pallas_call | solution.py:169
  713.4 22.2 %all_to_all.21 = bf16[8,384,128]{2,1,0:T(8,128)(2,1)} all-to-all(bf16[8,384,128]{2,1,0:T(8,128)(2,1)} %global_attention.2), channel_id=1, replica_groups=mesh['rep'=1,'tp'=4,'sp'=8] {'sp'}, dimensions={0} | all-to-all | bytes 1572864 | tf_op jit(solution)/shard_map/all_to_all | solution.py:402
  736.3 38.3 %global_attention.3 = bf16[8,384,128]{2,1,0:T(8,128)(2,1)} custom-call(bf16[8,3,384,128]{3,2,1,0:T(8,128)(2,1)} %all_to_all.20.q_ref, bf16[8,768,128]{2,1,0:T(8,128)(2,1)} %pad_maximum_fusion.1.k_ref, bf16[8,768,128]{2,1,0:T(8,128)(2,1)} %pad_maximum_fusion.2.v_ref), custom_call_target="tpu_custom_call" | custom-call | flops 9663676416 | bytes 6291456 | tf_op jit(solution)/shard_map/global_attention/pallas_call | solution.py:169
  774.5 16.7 %all_to_all.22 = bf16[8,384,128]{2,1,0:T(8,128)(2,1)} all-to-all(bf16[8,384,128]{2,1,0:T(8,128)(2,1)} %global_attention.3), channel_id=1, replica_groups=mesh['rep'=1,'tp'=4,'sp'=8] {'sp'}, dimensions={0} | all-to-all | bytes 1572864 | tf_op jit(solution)/shard_map/all_to_all | solution.py:402
  802.8 21.8 %psum.30.square_ref = f32[384,1]{1,0:T(8,128)} all-reduce(f32[384,1]{1,0:T(8,128)S(1)} %reshape.77), channel_id=1, replica_groups=mesh['rep'=1,'tp'=4,'sp'=8] {'tp'}, use_global_device_ids=true, to_apply=%region_8.9 | all-reduce | flops 384 | bytes 3072 | tf_op jit(solution)/shard_map/psum | solution.py:354
  843.3 19.8 %psum.31.square_ref = f32[384,1]{1,0:T(8,128)} all-reduce(f32[384,1]{1,0:T(8,128)S(1)} %reshape.78), channel_id=1, replica_groups=mesh['rep'=1,'tp'=4,'sp'=8] {'tp'}, use_global_device_ids=true, to_apply=%region_11.12 | all-reduce | flops 384 | bytes 3072 | tf_op jit(solution)/shard_map/psum | solution.py:354
  886.2 23.7 %fusion.10 = f32[384,3584]{1,0:T(8,128)} fusion(bf16[384,5120]{1,0:T(8,128)(2,1)} %norm_columns.10, bf16[2,5120,3584]{2,1,0:T(8,128)(2,1)} %param.17), kind=kOutput, calls=%fused_computation.10 | convolution fusion | flops 14092861440 | bytes 46137344 | tf_op jit(solution)/shard_map/dot_general | solution.py:308
  909.9 22.5 %fusion.65.clone.2 = bf16[384,3584]{1,0:T(8,128)(2,1)} fusion(bf16[384,5120]{1,0:T(8,128)(2,1)S(1)} %copy-done.7, bf16[2,5120,3584]{2,1,0:T(8,128)(2,1)} %param.18, f32[384,3584]{1,0:T(8,128)} %fusion.10), kind=kOutput, calls=%fused_computation.56.clone.clone.clone | convolution fusion | flops 14101118976 | bytes 48889856 | tf_op jit(solution)/shard_map/dot_general | solution.py:308
  932.4 22.7 %fusion.2 = f32[384,5120]{1,0:T(8,128)} fusion(bf16[2,3584,5120]{2,1,0:T(8,128)(2,1)} %param.19, bf16[384,3584]{1,0:T(8,128)(2,1)} %fusion.65.clone.2), kind=kOutput, calls=%fused_computation.2 | convolution fusion | flops 14092861440 | bytes 47316992 | tf_op jit(solution)/shard_map/dot_general | solution.py:308
  961.7 23.0 %fusion.8 = f32[384,3584]{1,0:T(8,128)} fusion(bf16[384,5120]{1,0:T(8,128)(2,1)} %norm_columns.11, bf16[2,5120,3584]{2,1,0:T(8,128)(2,1)} %param.17), kind=kOutput, calls=%fused_computation.8 | convolution fusion | flops 14092861440 | bytes 46137344 | tf_op jit(solution)/shard_map/dot_general | solution.py:308
  984.7 22.7 %fusion.60.clone.5 = bf16[384,3584]{1,0:T(8,128)(2,1)} fusion(bf16[384,5120]{1,0:T(8,128)(2,1)S(1)} %copy-done.5, bf16[2,5120,3584]{2,1,0:T(8,128)(2,1)} %param.18, f32[384,3584]{1,0:T(8,128)} %fusion.8), kind=kOutput, calls=%fused_computation.55.clone.clone.clone.2 | convolution fusion | flops 14101118976 | bytes 48889856 | tf_op jit(solution)/shard_map/dot_general | solution.py:308
  1007.4 22.5 %fusion = f32[384,5120]{1,0:T(8,128)} fusion(bf16[2,3584,5120]{2,1,0:T(8,128)(2,1)} %param.19, bf16[384,3584]{1,0:T(8,128)(2,1)} %fusion.60.clone.5), kind=kOutput, calls=%fused_computation | convolution fusion | flops 14092861440 | bytes 47316992 | tf_op jit(solution)/shard_map/dot_general | solution.py:308
  1030.7 73.2 %reduce-scatter.11.cloned.1.call-done.sum_ref = f32[96,5120]{1,0:T(8,128)} async-done(((f32[384,5120]{1,0:T(8,128)}), f32[96,5120]{1,0:T(8,128)}) %reduce-scatter.11.cloned.1.call-update) | async-done | bytes 1966096 | tf_op jit(solution)/shard_map/reduce_scatter | solution.py:328
  1108.0 72.1 %reduce-scatter.9.cloned.1.call-done.sum_ref = f32[96,5120]{1,0:T(8,128)} async-done(((f32[384,5120]{1,0:T(8,128)}), f32[96,5120]{1,0:T(8,128)}) %reduce-scatter.9.cloned.1.call-update) | async-done | bytes 1966096 | tf_op jit(solution)/shard_map/reduce_scatter | solution.py:328
  1184.9 40.4 %all-gather.35.cloned.1.call-done = bf16[384,5120]{1,0:T(8,128)(2,1)} async-done(((bf16[96,5120]{1,0:T(8,128)(2,1)}), bf16[384,5120]{1,0:T(8,128)(2,1)}) %all-gather.35.cloned.1.call-update) | async-done | bytes 3932176 | tf_op jit(solution)/shard_map/all_gather | solution.py:331
  1225.3 45.4 %all-gather.33.cloned.1.call-done = bf16[384,5120]{1,0:T(8,128)(2,1)} async-done(((bf16[96,5120]{1,0:T(8,128)(2,1)}), bf16[384,5120]{1,0:T(8,128)(2,1)}) %all-gather.33.cloned.1.call-update) | async-done | bytes 3932176 | tf_op jit(solution)/shard_map/all_gather | solution.py:331
  (196 shorter events, 309.4 us)
Async XLA Ops:
  7.2 86.8 %all-gather.37.cloned.1.call-start = ((), (), s32[]{:S(2)}) async-start(), calls=%async_computation.18 | async-start | bytes 4718592 | tf_op jit(solution)/shard_map/all_gather | solution.py:378
  10.6 38.3 %collective-permute-start.2 = (bf16[1,128,1280]{2,1,0:T(8,128)(2,1)}, bf16[1,128,1280]{2,1,0:T(8,128)(2,1)}, u32[]{:S(2)}, u32[]{:S(2)}) collective-permute-start(bf16[1,128,1280]{2,1,0:T(8,128)(2,1)} %get-tuple-element.63), channel_id=1, source_target_pairs={{0,24},{8,0},{16,8},{24,16},{1,25},{9,1},{17,9},{25,17},{2,26},{10... | collective-permute-start | bytes 983048 | tf_op jit(solution)/shard_map/ppermute | solution.py:343
  15.8 39.3 %collective-permute-start.1 = (bf16[1,128,1280]{2,1,0:T(8,128)(2,1)}, bf16[1,128,1280]{2,1,0:T(8,128)(2,1)}, u32[]{:S(2)}, u32[]{:S(2)}) collective-permute-start(bf16[1,128,1280]{2,1,0:T(8,128)(2,1)} %get-tuple-element.64), channel_id=1, source_target_pairs={{0,16},{8,24},{16,0},{24,8},{1,17},{9,25},{17,1},{25,9},{2,18},{10... | collective-permute-start | bytes 983048 | tf_op jit(solution)/shard_map/ppermute | solution.py:343
  15.8 39.3 %collective-permute-start = (bf16[1,128,1280]{2,1,0:T(8,128)(2,1)}, bf16[1,128,1280]{2,1,0:T(8,128)(2,1)}, u32[]{:S(2)}, u32[]{:S(2)}) collective-permute-start(bf16[1,128,1280]{2,1,0:T(8,128)(2,1)} %get-tuple-element.65), channel_id=1, source_target_pairs={{0,8},{8,16},{16,24},{24,0},{1,9},{9,17},{17,25},{25,1},{2,10},{10... | collective-permute-start | bytes 983048 | tf_op jit(solution)/shard_map/ppermute | solution.py:343
  16.5 41.1 %collective-permute-start.5 = (bf16[1,128,1280]{2,1,0:T(8,128)(2,1)}, bf16[1,128,1280]{2,1,0:T(8,128)(2,1)}, u32[]{:S(2)}, u32[]{:S(2)}) collective-permute-start(bf16[1,128,1280]{2,1,0:T(8,128)(2,1)} %get-tuple-element.67), channel_id=1, source_target_pairs={{0,24},{8,0},{16,8},{24,16},{1,25},{9,1},{17,9},{25,17},{2,26},{10... | collective-permute-start | bytes 983048 | tf_op jit(solution)/shard_map/ppermute | solution.py:343
  18.5 39.1 %collective-permute-start.4 = (bf16[1,128,1280]{2,1,0:T(8,128)(2,1)}, bf16[1,128,1280]{2,1,0:T(8,128)(2,1)}, u32[]{:S(2)}, u32[]{:S(2)}) collective-permute-start(bf16[1,128,1280]{2,1,0:T(8,128)(2,1)} %get-tuple-element.68), channel_id=1, source_target_pairs={{0,16},{8,24},{16,0},{24,8},{1,17},{9,25},{17,1},{25,9},{2,18},{10... | collective-permute-start | bytes 983048 | tf_op jit(solution)/shard_map/ppermute | solution.py:343
  48.9 8.6 collective-permute-start.3
  60.9 91.7 %all-gather.25.cloned.1.call-start = ((), (), s32[]{:S(2)}) async-start(), calls=%async_computation.8 | async-start | bytes 11796480 | tf_op jit(solution)/shard_map/all_gather | solution.py:348
  61.7 130.5 %all-gather.39.cloned.1.call-start = ((), (), s32[]{:S(2)}) async-start(), calls=%async_computation.19 | async-start | bytes 3932160 | tf_op jit(solution)/shard_map/all_gather | solution.py:351
  61.8 16.3 %collective-permute-start.6 = (bf16[2,2,512,128]{3,2,1,0:T(8,128)(2,1)}, bf16[2,2,512,128]{3,2,1,0:T(8,128)(2,1)S(1)}, u32[]{:S(2)}, u32[]{:S(2)}) collective-permute-start(bf16[2,2,512,128]{3,2,1,0:T(8,128)(2,1)} %pad_maximum_fusion.7), channel_id=1, source_target_pairs={{0,1},{1,2},{2,3},{3,4},{4,5},{5,6},{6,7},{8,9},{9,10},{10,11},{11... | collective-permute-start | bytes 1572872 | tf_op jit(solution)/shard_map/ppermute | solution.py:372
  155.3 79.1 %all-gather.43.cloned.1.call-start = ((), (), s32[]{:S(2)}) async-start(), calls=%async_computation.21 | async-start | bytes 3932160 | tf_op jit(solution)/shard_map/all_gather | solution.py:351
  156.0 126.8 %all-gather.41.cloned.1.call-start = ((), (), s32[]{:S(2)}) async-start(), calls=%async_computation.20 | async-start | bytes 4915200 | tf_op jit(solution)/shard_map/all_gather | solution.py:356
  227.3 131.3 %all-gather.45.cloned.1.call-start = ((), (), s32[]{:S(2)}) async-start(), calls=%async_computation.22 | async-start | bytes 4915200 | tf_op jit(solution)/shard_map/all_gather | solution.py:356
  269.5 164.3 %reduce-scatter.5.cloned.1.call-start = ((), (), s32[]{:S(2)}) async-start(), calls=%async_computation.9 | async-start | bytes 9830400 | tf_op jit(solution)/shard_map/reduce_scatter | solution.py:328
  358.5 150.6 %reduce-scatter.7.cloned.1.call-start = ((), (), s32[]{:S(2)}) async-start(), calls=%async_computation.11 | async-start | bytes 9830400 | tf_op jit(solution)/shard_map/reduce_scatter | solution.py:328
  433.7 120.7 %all-gather.27.cloned.1.call-start = ((), (), s32[]{:S(2)}) async-start(), calls=%async_computation.10 | async-start | bytes 4915200 | tf_op jit(solution)/shard_map/all_gather | solution.py:331
  437.8 75.3 %copy-start.10 = (f32[768,64]{1,0:T(8,128)S(1)}, f32[768,64]{1,0:T(8,128)}, u32[]{:S(2)}) copy-start(f32[768,64]{1,0:T(8,128)} %get-tuple-element.91) | copy-start | bytes 589828
  437.8 75.3 %copy-start.11 = (f32[768,64]{1,0:T(8,128)S(1)}, f32[768,64]{1,0:T(8,128)}, u32[]{:S(2)}) copy-start(f32[768,64]{1,0:T(8,128)} %get-tuple-element.92) | copy-start | bytes 589828
  437.9 75.3 %copy-start.12 = (f32[768,64]{1,0:T(8,128)S(1)}, f32[768,64]{1,0:T(8,128)}, u32[]{:S(2)}) copy-start(f32[768,64]{1,0:T(8,128)} %get-tuple-element.93) | copy-start | bytes 589828
  437.9 162.3 %all-gather.29.cloned.1.call-start = ((), (), s32[]{:S(2)}) async-start(), calls=%async_computation.12 | async-start | bytes 4915200 | tf_op jit(solution)/shard_map/all_gather | solution.py:331
  579.4 34.2 %all-to-all-start = ((bf16[8,3,384,128]{3,2,1,0:T(8,128)(2,1)}), bf16[8,3,384,128]{3,2,1,0:T(8,128)(2,1)S(1)}, u32[]{:S(2)}, u32[]{:S(2)}) async-start(bf16[8,3,384,128]{3,2,1,0:T(8,128)(2,1)} %rope_send.2), calls=%async_computation.1 | async-start | bytes 4718592 | tf_op jit(solution)/shard_map/all_to_all | solution.py:393
  584.5 151.6 %all-gather.31.cloned.1.call-start = ((), (), s32[]{:S(2)}) async-start(), calls=%async_computation.13 | async-start | bytes 11796480 | tf_op jit(solution)/shard_map/all_gather | solution.py:348
  613.5 60.2 %copy-start = (bf16[8,3,384,128]{3,2,1,0:T(8,128)(2,1)}, bf16[8,3,384,128]{3,2,1,0:T(8,128)(2,1)S(1)}, u32[]{:S(2)}) copy-start(bf16[8,3,384,128]{3,2,1,0:T(8,128)(2,1)S(1)} %all-to-all-done.q_ref) | copy-start | bytes 7077892
  673.6 117.7 %all-gather.47.cloned.1.call-start = ((), (), s32[]{:S(2)}) async-start(), calls=%async_computation.23 | async-start | bytes 3932160 | tf_op jit(solution)/shard_map/all_gather | solution.py:351
  736.2 95.6 %all-gather.51.cloned.1.call-start = ((), (), s32[]{:S(2)}) async-start(), calls=%async_computation.25 | async-start | bytes 3932160 | tf_op jit(solution)/shard_map/all_gather | solution.py:351
  791.3 88.3 %all-gather.49.cloned.1.call-start = ((), (), s32[]{:S(2)}) async-start(), calls=%async_computation.24 | async-start | bytes 4915200 | tf_op jit(solution)/shard_map/all_gather | solution.py:356
  828.5 126.6 %all-gather.53.cloned.1.call-start = ((), (), s32[]{:S(2)}) async-start(), calls=%async_computation.26 | async-start | bytes 4915200 | tf_op jit(solution)/shard_map/all_gather | solution.py:356
  866.9 237.0 %reduce-scatter.11.cloned.1.call-start = ((), (), s32[]{:S(2)}) async-start(), calls=%async_computation.16 | async-start | bytes 9830400 | tf_op jit(solution)/shard_map/reduce_scatter | solution.py:328
  1030.0 150.2 %reduce-scatter.9.cloned.1.call-start = ((), (), s32[]{:S(2)}) async-start(), calls=%async_computation.14 | async-start | bytes 9830400 | tf_op jit(solution)/shard_map/reduce_scatter | solution.py:328
  1030.6 194.6 %all-gather.35.cloned.1.call-start = ((), (), s32[]{:S(2)}) async-start(), calls=%async_computation.17 | async-start | bytes 4915200 | tf_op jit(solution)/shard_map/all_gather | solution.py:331
  1107.9 76.2 %copy-start.17 = (bf16[2,512,128]{2,1,0:T(8,128)(2,1)S(1)}, bf16[2,512,128]{2,1,0:T(8,128)(2,1)}, u32[]{:S(2)}) copy-start(bf16[2,512,128]{2,1,0:T(8,128)(2,1)} %dynamic-slice_bitcast_fusion.6) | copy-start | bytes 786436
  1107.9 162.7 %all-gather.33.cloned.1.call-start = ((), (), s32[]{:S(2)}) async-start(), calls=%async_computation.15 | async-start | bytes 4915200 | tf_op jit(solution)/shard_map/all_gather | solution.py:331
  (26 other events, 246.9 us)
Sparse Core Ops, SparseCore 0:
  61.0 32.9 all-gather.36
  96.2 56.3 all-gather.24
  155.5 36.6 all-gather.38
  193.6 40.7 all-gather.42
  236.4 46.2 all-gather.40
  284.8 42.7 all-gather.44
  358.6 73.5 reduce-scatter.4
  435.1 73.9 reduce-scatter.6
  511.2 43.0 all-gather.26
  556.4 43.7 all-gather.28
  673.7 62.3 all-gather.30
  737.5 36.4 all-gather.46
  791.4 40.3 all-gather.50
  833.2 46.2 all-gather.48
  880.9 42.7 all-gather.52
  1030.1 73.7 reduce-scatter.10
  1106.1 73.9 reduce-scatter.8
  1182.1 43.0 all-gather.34
  1226.8 43.7 all-gather.32
